TPU v7x, 32 devices: a whole 2x2x4 slice. The times are simulated.
32 devices in a mesh: dp: 4 (over y, core), vocab: 8 (over z, x).
Axes of the slice: x: 2, y: 2, z: 4, core: 2. Of those that a mesh axis runs over, the one named last changes fastest.
Arguments:
- hidden: bfloat16 [256, 3584], P('dp'), may hold values from -48 to 48
- embedding: bfloat16 [24576, 3584], P(('dp', 'vocab')), may hold values from -1 to 1
- targets: int32 [256], P('dp'), may hold values from 0 to 24575
- loss_weight: bfloat16 [256], P('dp'), may hold values from 1 to 10
Outputs:
- hidden_grad: bfloat16 [256, 3584], P('dp')
- table_grad: bfloat16 [24576, 3584], P(('dp', 'vocab'))
All inputs are finite; a program needn't handle non-finite values.
Results may differ from a plain program's by a relative error of at most 0.0049.
Values may be sent and summed in bfloat16 or wider, within the bound.
A program may use at most 128 MiB of HBM per device.

v0:
```python
import jax
import jax.numpy as jnp
from jax import lax
from jax.sharding import PartitionSpec as P

soft_cap = 30.0
z_weight = 0.002


def body(hidden, embedding, targets, loss_weight):
    shard_rows = embedding.shape[0]
    group_hidden, group_weight = (
        lax.all_gather(hidden, "dp", axis=0, tiled=True),
        lax.all_gather(loss_weight, "dp", axis=0, tiled=True),
    )
    group_targets = lax.all_gather(targets, "dp", axis=0, tiled=True)
    logits = lax.dot_general(
        group_hidden, embedding, (((1,), (1,)), ((), ())), preferred_element_type=jnp.float32
    )
    capped = soft_cap * jnp.tanh(logits / soft_cap)
    exp_terms = jnp.exp(capped - soft_cap)
    partial_value = jnp.sum(exp_terms, axis=1)
    weight = group_weight.astype(jnp.float32)
    device_place = lax.axis_index("dp") * lax.axis_size("vocab") + lax.axis_index("vocab")
    exp_total = lax.psum(partial_value, ("dp", "vocab"))
    factor = weight * (1.0 + 2.0 * z_weight * (soft_cap + jnp.log(exp_total))) / exp_total
    columns = device_place * shard_rows + lax.iota(jnp.int32, shard_rows)
    target_hit = group_targets[:, None] == columns[None, :]
    softmax_part = factor[:, None] * exp_terms - jnp.where(target_hit, weight[:, None], 0.0)
    scores_grad = (softmax_part * (1.0 - (capped / soft_cap) ** 2)).astype(jnp.bfloat16)
    table_grad = lax.dot_general(
        scores_grad, group_hidden, (((0,), (0,)), ((), ())), preferred_element_type=jnp.float32
    ).astype(jnp.bfloat16)
    group_grad = lax.psum_scatter(
        jnp.dot(scores_grad, embedding, preferred_element_type=jnp.float32),
        "dp",
        scatter_dimension=0,
        tiled=True,
    )
    hidden_grad = lax.psum(group_grad, "vocab").astype(jnp.bfloat16)
    return (hidden_grad, table_grad)


def solution(mesh):
    return jax.shard_map(
        body,
        mesh=mesh,
        in_specs=(P("dp", None), P(("dp", "vocab"), None), P("dp"), P("dp")),
        out_specs=(P("dp", None), P(("dp", "vocab"), None)),
        check_vma=False,
    )
```

profile of v0, /device:TPU:0, one launch (start us, length us, event | category | flops | bytes accessed | tf_op | source)
XLA Modules:
  0.0 182.5 jit_solution(10813239611045289594)
XLA Ops:
  7.2 0.0 all-gather.2.cloned.1.call-start
  7.2 0.7 all-gather.2.cloned.1.call-update
  7.9 0.0 reduce-scatter.2.cloned.1.call-start
  8.0 1.2 dynamic-slice
  9.9 0.9 dynamic-update-slice
  10.7 8.4 %all-reduce = bf16[256]{0:T(256)(128)(2,1)S(1)} all-reduce(bf16[256]{0:T(256)(128)(2,1)S(1)} %dynamic-update-slice), channel_id=1, replica_groups=mesh['dp'=4,'vocab'=8] {'dp'}, use_global_device_ids=true, to_apply=%add | all-reduce | flops 256 | bytes 1024
  19.1 0.9 dynamic-update-slice.1
  20.0 4.5 %all-reduce.1 = s32[256]{0:T(256)S(1)} all-reduce(s32[256]{0:T(256)S(1)} %dynamic-update-slice.1), channel_id=1, replica_groups=mesh['dp'=4,'vocab'=8] {'dp'}, use_global_device_ids=true, to_apply=%add.1 | all-reduce | flops 256 | bytes 2048
  24.4 9.0 %all-gather.2.cloned.1.call-done = bf16[256,3584]{1,0:T(8,128)(2,1)} async-done(((bf16[64,3584]{1,0:T(8,128)(2,1)}), bf16[256,3584]{1,0:T(8,128)(2,1)}) %all-gather.2.cloned.1.call-update) | async-done | bytes 1835024 | tf_op jit(solution)/shard_map/all_gather | solution.py:13
  33.5 4.9 %fusion.1 = (f32[256]{0:T(256)S(1)}, f32[256,768]{1,0:T(8,128)S(1)}) fusion(bf16[256,3584]{1,0:T(8,128)(2,1)} %all-gather.2.cloned.1.call-done, bf16[768,3584]{1,0:T(8,128)(2,1)} %param.5), kind=kOutput, calls=%fused_computation.5 | convolution fusion | flops 1410072320 | bytes 8127488 | tf_op jit(solution)/shard_map/dot_general | solution.py:17
  38.4 39.3 %psum.14 = f32[256]{0:T(256)S(1)} all-reduce(f32[256]{0:T(256)S(1)} %get-tuple-element.2), channel_id=1, replica_groups=mesh['dp'=4,'vocab'=8] {'dp','vocab'}, use_global_device_ids=true, to_apply=%region_1.0 | all-reduce | flops 256 | bytes 2048 | tf_op jit(solution)/shard_map/psum | solution.py:25
  77.7 0.0 copy-start
  77.7 6.3 %fusion.2 = f32[256,3584]{1,0:T(8,128)} fusion(bf16[768,3584]{1,0:T(8,128)(2,1)} %param.5, f32[256,768]{1,0:T(8,128)S(1)} %get-tuple-element.3, f32[256]{0:T(256)S(1)} %convert_element_type.12, s32[768]{0:T(1024)S(1)} %iota_add_fusion, f32[256]{0:T(256)S(1)} %multiply_divide_fusion, s32[256]{0:T(256)S(1)} %all-reduce.1), kind=kOutput, calls=%fused_computation.8 | convolution fusion | flops 1411252224 | bytes 9967616 | tf_op jit(solution)/shard_map/dot_general | solution.py:35
  84.0 0.0 reduce-scatter.2.cloned.1.call-update
  84.0 0.0 copy-done
  84.0 4.3 %convolution_convert_fusion = bf16[768,3584]{1,0:T(8,128)(2,1)} fusion(bf16[256,3584]{1,0:T(8,128)(2,1)S(1)} %copy-done, f32[256,768]{1,0:T(8,128)S(1)} %get-tuple-element.3, f32[256]{0:T(256)S(1)} %convert_element_type.12, s32[768]{0:T(1024)S(1)} %iota_add_fusion, f32[256]{0:T(256)S(1)} %multiply_divide_fusion, s32[256]{0:T(256)S(1)} %all-reduce.1), kind=kOutput, calls=%fused_computation | convolution fusion | flops 1414004736 | bytes 8132608 | tf_op jit(solution)/shard_map/dot_general | solution.py:31
  88.3 37.9 %reduce-scatter.2.cloned.1.call-done = f32[64,3584]{1,0:T(8,128)} async-done(((f32[256,3584]{1,0:T(8,128)}), f32[64,3584]{1,0:T(8,128)}) %reduce-scatter.2.cloned.1.call-update) | async-done | bytes 917520 | tf_op jit(solution)/shard_map/reduce_scatter | solution.py:34
  126.2 49.4 %all-reduce.3 = bf16[64,3584]{1,0:T(8,128)(2,1)} all-reduce(f32[64,3584]{1,0:T(8,128)} %reduce-scatter.2.cloned.1.call-done), channel_id=1, replica_groups=mesh['dp'=4,'vocab'=8] {'vocab'}, use_global_device_ids=true, to_apply=%region_3.4 | all-reduce | flops 229376 | bytes 1376256 | tf_op jit(solution)/shard_map/psum | solution.py:40
  (5 shorter events, 0.0 us)
Async XLA Ops:
  7.2 26.3 %all-gather.2.cloned.1.call-start = ((), (), s32[]{:S(2)}) async-start(), calls=%async_computation.1 | async-start | bytes 2293760 | tf_op jit(solution)/shard_map/all_gather | solution.py:13
  7.9 118.3 %reduce-scatter.2.cloned.1.call-start = ((), (), s32[]{:S(2)}) async-start(), calls=%async_computation.2 | async-start | bytes 4587520 | tf_op jit(solution)/shard_map/reduce_scatter | solution.py:34
  77.7 6.3 %copy-start = (bf16[256,3584]{1,0:T(8,128)(2,1)S(1)}, bf16[256,3584]{1,0:T(8,128)(2,1)}, u32[]{:S(2)}) copy-start(bf16[256,3584]{1,0:T(8,128)(2,1)} %all-gather.2.cloned.1.call-done) | copy-start | bytes 5505028
Sparse Core Ops, SparseCore 0:
  9.5 23.9 all-gather.1
  84.1 42.0 reduce-scatter.1
where the time goes:
time: 183 us; the launch traced here: 182 us
  blocking collectives  102 us (56%)
  waiting for transfers between devices  47.6 us (26%)
  matrix products  15.4 us (8%)
  between operations  14.7 us (8%)
  local copies, waits for them, and re-layouts  2.97 us (2%)
    psum x1, blocking collectives, body(): hidden_grad = lax.psum(group_grad, 'vocab').astype(jnp.bfloat16)  49.4 us
    psum x1, blocking collectives, body(): exp_total = lax.psum(partial_value, ('dp', 'vocab'))  39.3 us
    reduce_scatter x1, waiting for transfers between devices, body(): lax.psum_scatter(jnp.dot(scores_grad, embedding, preferred_element_type=j...  37.9 us
    unnamed x2, blocking collectives  12.8 us
    all_gather x1, waiting for transfers between devices, body(): lax.all_gather(hidden, 'dp', axis=0, tiled=True)  9.04 us
    dot_general x1, matrix products, body(): jnp.dot(scores_grad, embedding, preferred_element_type=jnp.float32)  6.28 us
    dot_general x1, matrix products, body(): lax.dot_general(group_hidden, embedding, (((1,), (1,)), ((), ())), prefer...  4.91 us
    dot_general x1, matrix products, body(): lax.dot_general(scores_grad, group_hidden, (((0,), (0,)), ((), ())), pref...  4.26 us
  transfers between devices with their start and end apart: 2, of which 2 were waited for; matrix products, arithmetic and copies ran while one was open for 4% of the time, Pallas kernels for 0%

commit v1 on v0

--- a/solution.py
+++ b/solution.py
@@ -22,7 +22,8 @@
     partial_value = jnp.sum(exp_terms, axis=1)
     weight = group_weight.astype(jnp.float32)
     device_place = lax.axis_index("dp") * lax.axis_size("vocab") + lax.axis_index("vocab")
-    exp_total = lax.psum(partial_value, ("dp", "vocab"))
+    half = lax.psum(partial_value, "vocab")
+    exp_total = lax.psum(half, "dp")
     factor = weight * (1.0 + 2.0 * z_weight * (soft_cap + jnp.log(exp_total))) / exp_total
     columns = device_place * shard_rows + lax.iota(jnp.int32, shard_rows)
     target_hit = group_targets[:, None] == columns[None, :]

time: 183 us -> 166 us (0.907)
  blocking collectives: 102 us -> 89.5 us
  waiting for transfers between devices: 47.6 us -> 42.8 us
    psum x1 -> x2, blocking collectives: 39.3 us -> 27.3 us  [the longest x1 21.4 us: body(): half = lax.psum(partial_value, 'vocab')]
    reduce_scatter x1, waiting for transfers between devices: 37.9 us -> 33.1 us  [body(): lax.psum_scatter(jnp.dot(scores_grad, embedding, preferred_element_type=j...]
where the time goes in v1:
time: 166 us
  blocking collectives  89.5 us (54%)
  waiting for transfers between devices  42.8 us (26%)
  matrix products  15.5 us (9%)
  between operations  14.7 us (9%)
  local copies, waits for them, and re-layouts  2.97 us (2%)
    psum x1, blocking collectives, body(): hidden_grad = lax.psum(group_grad, 'vocab').astype(jnp.bfloat16)  49.4 us
    reduce_scatter x1, waiting for transfers between devices, body(): lax.psum_scatter(jnp.dot(scores_grad, embedding, preferred_element_type=j...  33.1 us
    psum x1, blocking collectives, body(): half = lax.psum(partial_value, 'vocab')  21.4 us
    unnamed x2, blocking collectives  12.8 us
    all_gather x1, waiting for transfers between devices, body(): lax.all_gather(hidden, 'dp', axis=0, tiled=True)  9.04 us
    dot_general x1, matrix products, body(): jnp.dot(scores_grad, embedding, preferred_element_type=jnp.float32)  6.28 us
    psum x1, blocking collectives, body(): exp_total = lax.psum(half, 'dp')  5.91 us
    dot_general x1, matrix products, body(): lax.dot_general(group_hidden, embedding, (((1,), (1,)), ((), ())), prefer...  4.91 us
  transfers between devices with their start and end apart: 2, of which 2 were waited for; matrix products, arithmetic and copies ran while one was open for 4% of the time, Pallas kernels for 0%

profile of v1, /device:TPU:0, one launch (start us, length us, event | category | flops | bytes accessed | tf_op | source)
XLA Modules:
  0.0 165.6 jit_solution(14732195251972896261)
XLA Ops:
  7.2 0.0 all-gather.2.cloned.1.call-start
  7.2 0.7 all-gather.2.cloned.1.call-update
  7.9 0.0 reduce-scatter.2.cloned.1.call-start
  8.0 1.2 dynamic-slice
  9.9 0.9 dynamic-update-slice
  10.7 8.4 %all-reduce = bf16[256]{0:T(256)(128)(2,1)S(1)} all-reduce(bf16[256]{0:T(256)(128)(2,1)S(1)} %dynamic-update-slice), channel_id=1, replica_groups=mesh['dp'=4,'vocab'=8] {'dp'}, use_global_device_ids=true, to_apply=%add | all-reduce | flops 256 | bytes 1024
  19.1 0.9 dynamic-update-slice.1
  20.0 4.5 %all-reduce.1 = s32[256]{0:T(256)S(1)} all-reduce(s32[256]{0:T(256)S(1)} %dynamic-update-slice.1), channel_id=1, replica_groups=mesh['dp'=4,'vocab'=8] {'dp'}, use_global_device_ids=true, to_apply=%add.1 | all-reduce | flops 256 | bytes 2048
  24.4 9.0 %all-gather.2.cloned.1.call-done = bf16[256,3584]{1,0:T(8,128)(2,1)} async-done(((bf16[64,3584]{1,0:T(8,128)(2,1)}), bf16[256,3584]{1,0:T(8,128)(2,1)}) %all-gather.2.cloned.1.call-update) | async-done | bytes 1835024 | tf_op jit(solution)/shard_map/all_gather | solution.py:13
  33.5 4.9 %fusion.1 = (f32[256]{0:T(256)S(1)}, f32[256,768]{1,0:T(8,128)S(1)}) fusion(bf16[256,3584]{1,0:T(8,128)(2,1)} %all-gather.2.cloned.1.call-done, bf16[768,3584]{1,0:T(8,128)(2,1)} %param.5), kind=kOutput, calls=%fused_computation.5 | convolution fusion | flops 1410072320 | bytes 8127488 | tf_op jit(solution)/shard_map/dot_general | solution.py:17
  38.4 21.4 %psum.21 = f32[256]{0:T(256)S(1)} all-reduce(f32[256]{0:T(256)S(1)} %get-tuple-element.2), channel_id=1, replica_groups=mesh['dp'=4,'vocab'=8] {'vocab'}, use_global_device_ids=true, to_apply=%region_1.0 | all-reduce | flops 256 | bytes 2048 | tf_op jit(solution)/shard_map/psum | solution.py:25
  59.7 5.9 %psum.22 = f32[256]{0:T(256)S(1)} all-reduce(f32[256]{0:T(256)S(1)} %psum.21), channel_id=1, replica_groups=mesh['dp'=4,'vocab'=8] {'dp'}, use_global_device_ids=true, to_apply=%region_2.0 | all-reduce | flops 256 | bytes 2048 | tf_op jit(solution)/shard_map/psum | solution.py:26
  65.7 0.0 copy-start
  65.7 6.3 %fusion.2 = f32[256,3584]{1,0:T(8,128)} fusion(bf16[768,3584]{1,0:T(8,128)(2,1)} %param.5, f32[256,768]{1,0:T(8,128)S(1)} %get-tuple-element.3, f32[256]{0:T(256)S(1)} %convert_element_type.12, s32[768]{0:T(1024)S(1)} %iota_add_fusion, f32[256]{0:T(256)S(1)} %multiply_divide_fusion, s32[256]{0:T(256)S(1)} %all-reduce.1), kind=kOutput, calls=%fused_computation.8 | convolution fusion | flops 1411252224 | bytes 9967616 | tf_op jit(solution)/shard_map/dot_general | solution.py:36
  72.0 0.0 reduce-scatter.2.cloned.1.call-update
  72.0 0.0 copy-done
  72.0 4.3 %convolution_convert_fusion = bf16[768,3584]{1,0:T(8,128)(2,1)} fusion(bf16[256,3584]{1,0:T(8,128)(2,1)S(1)} %copy-done, f32[256,768]{1,0:T(8,128)S(1)} %get-tuple-element.3, f32[256]{0:T(256)S(1)} %convert_element_type.12, s32[768]{0:T(1024)S(1)} %iota_add_fusion, f32[256]{0:T(256)S(1)} %multiply_divide_fusion, s32[256]{0:T(256)S(1)} %all-reduce.1), kind=kOutput, calls=%fused_computation | convolution fusion | flops 1414004736 | bytes 8132608 | tf_op jit(solution)/shard_map/dot_general | solution.py:32
  76.3 33.1 %reduce-scatter.2.cloned.1.call-done = f32[64,3584]{1,0:T(8,128)} async-done(((f32[256,3584]{1,0:T(8,128)}), f32[64,3584]{1,0:T(8,128)}) %reduce-scatter.2.cloned.1.call-update) | async-done | bytes 917520 | tf_op jit(solution)/shard_map/reduce_scatter | solution.py:35
  109.4 49.4 %all-reduce.3 = bf16[64,3584]{1,0:T(8,128)(2,1)} all-reduce(f32[64,3584]{1,0:T(8,128)} %reduce-scatter.2.cloned.1.call-done), channel_id=1, replica_groups=mesh['dp'=4,'vocab'=8] {'vocab'}, use_global_device_ids=true, to_apply=%region_4.5 | all-reduce | flops 229376 | bytes 1376256 | tf_op jit(solution)/shard_map/psum | solution.py:41
  (5 shorter events, 0.0 us)
Async XLA Ops:
  7.2 26.3 %all-gather.2.cloned.1.call-start = ((), (), s32[]{:S(2)}) async-start(), calls=%async_computation.1 | async-start | bytes 2293760 | tf_op jit(solution)/shard_map/all_gather | solution.py:13
  7.9 101.5 %reduce-scatter.2.cloned.1.call-start = ((), (), s32[]{:S(2)}) async-start(), calls=%async_computation.2 | async-start | bytes 4587520 | tf_op jit(solution)/shard_map/reduce_scatter | solution.py:35
  65.7 6.3 %copy-start = (bf16[256,3584]{1,0:T(8,128)(2,1)S(1)}, bf16[256,3584]{1,0:T(8,128)(2,1)}, u32[]{:S(2)}) copy-start(bf16[256,3584]{1,0:T(8,128)(2,1)} %all-gather.2.cloned.1.call-done) | copy-start | bytes 5505028
Sparse Core Ops, SparseCore 0:
  9.5 23.9 all-gather.1
  72.1 37.2 reduce-scatter.1
